TPU v7x, 32 devices: a whole 2x2x4 slice. The times are simulated.
32 devices in a mesh: rows: 8 (over z, y), cols: 4 (over x, core).
Axes of the slice: x: 2, y: 2, z: 4, core: 2. Of those that a mesh axis runs over, the one named last changes fastest.
Arguments:
- matrix: bfloat16 [2048, 8192], P('rows', 'cols'), may hold values from -0.125 to 0.125
- inverse: bfloat16 [16384, 8192], P('rows', 'cols'), may hold values from -1 to 1
- target: float32 [2048, 128], P('rows'), may hold values from -60 to 60
- penalty: float32 [128], replicated, may hold values from 0.5 to 16
- consensus: float32 [8192, 128], P('cols'), may hold values from -6 to 6
- copy_duals: float32 [8, 8192, 128], P('rows', 'cols'), may hold values from -6 to 6
- fit_parts: float32 [4, 2048, 128], P('cols', 'rows'), may hold values from -6 to 6
- fit_mean: float32 [2048, 128], P('rows'), may hold values from -3 to 3
- fit_duals: float32 [2048, 128], P('rows'), may hold values from -3 to 3
Outputs:
- coefficients: float32 [8192, 128], P('cols')
- fitted: float32 [2048, 128], P('rows')
- history: float32 [5, 2], replicated
All inputs are finite; a program needn't handle non-finite values.
Results may differ from a plain program's by a relative error of at most 0.006.
Values sent between devices are 32-bit elements; how exact they have to be, the bound alone decides.
No kernel may reach another device: no remote copies, remote signals or barrier semaphores. Data moves between devices by JAX's collectives and lax.ppermute only.
A program may use at most 64 MiB of HBM per device.

v0:
```python
import functools

import jax
import jax.numpy as jnp
from jax import lax
from jax.experimental import pallas as pl
from jax.experimental.pallas import tpu as pltpu
from jax.sharding import PartitionSpec as P


ITERS = 5
STREAMS = 4
MERGED = 2
F32 = jnp.float32
BF16 = jnp.bfloat16


def bits_of(size):
    bits, bit = [], 1
    while bit < size:
        bits.append(bit)
        bit *= 2
    return bits


def swap(values, axis, size, bit):
    return lax.ppermute(values, axis, [(i, i ^ bit) for i in range(size)])


def butterfly(values, axis, size):
    for bit in bits_of(size):
        values = values + swap(values, axis, size, bit)
    return values


def fold(values):
    squares = values * values
    return jnp.sum(squares.reshape(-1, 8, squares.shape[-1]), axis=0)


def dot(a, b):
    return jnp.dot(a, b, preferred_element_type=F32)


def call(body, outs, *args, scratch=(), flops=0):
    return pl.pallas_call(
        body,
        out_shape=[jax.ShapeDtypeStruct(s, d) for s, d in outs],
        scratch_shapes=list(scratch),
        cost_estimate=pl.CostEstimate(flops=flops * 8, bytes_accessed=0, transcendentals=0),
        compiler_params=pltpu.CompilerParams(vmem_limit_bytes=8 * 1024 * 1024),
    )(*args)


def stage(inverse, out, sem):
    copy = pltpu.make_async_copy(inverse, out, sem)
    copy.start()
    copy.wait()


def first_offsets(cols, base, total, tall, out):
    offsets = base[...] - total[...] / cols
    out[...] = dot(tall[...], offsets.astype(BF16))


def next_offsets(cols, slot, shares, total, target, row_dual, tall, log, out, dual_out, log_out):
    mean_share = total[...] / cols
    fitted_mean = (target[...] + row_dual[...] + mean_share) / (cols + 1)
    dual = row_dual[...] + mean_share - fitted_mean
    offsets = shares[...] - mean_share + fitted_mean - dual
    out[...] = dot(tall[...], offsets.astype(BF16))
    dual_out[...] = dual
    log_out[...] = log[...]
    log_out[slot : slot + 8] += fold(mean_share - fitted_mean)


def last_fit(cols, slot, total, target, row_dual, log, out, log_out):
    mean_share = total[...] / cols
    fitted_mean = (target[...] + row_dual[...] + mean_share) / (cols + 1)
    out[...] = fitted_mean * cols
    log_out[...] = log[...]
    log_out[slot : slot + 8] += fold(mean_share - fitted_mean)


def first_copies(inverse, pulled, center, copy_dual, copies, *rest):
    *sums, right_side = rest
    right_side[...] = (center[...] - copy_dual[...] + pulled[...]).astype(BF16)
    rows = center.shape[0] // len(sums)
    for n, out in enumerate(sums):
        part = slice(n * rows, (n + 1) * rows)
        made = dot(inverse[part, :], right_side[...])
        copies[part, :] = made
        out[...] = made + copy_dual[part, :]


def block_of(ref, n, rows):
    return ref[...] if ref.shape[0] == rows else ref[n * rows : (n + 1) * rows, :]


def update(n, slot, total, plain, inverse, new, old, copies, copy_dual, pulled, log, *rest):
    rows = new.shape[0]
    part = slice(n * rows, (n + 1) * rows)
    gap = copies[part, :] - new[...]
    dual = block_of(copy_dual, n, rows) + gap
    right_side = (new[...] - dual + pulled[part, :]).astype(BF16)
    if n == 0:
        dual_out, log_out, out = rest
        out[...] = dot(inverse[:, part], right_side)
    elif n < total - 1:
        begun, dual_out, log_out, out = rest
        out[...] = begun[...] + dot(inverse[:, part], right_side)
    else:
        begun, others, (dual_out, log_out, out), sums = rest[0], rest[1:total], rest[total : total + 3], rest[total + 3 :]
        for m in range(total):
            block = slice(m * rows, (m + 1) * rows)
            made = begun[block, :] + dot(inverse[block, part], right_side)
            out[block, :] = made
            sums[m][...] = made if plain else made + (dual if m == n else others[m][...])
    dual_out[...] = dual
    log_out[...] = log[...]
    log_out[slot : slot + 8] += fold(gap)
    log_out[slot + 8 : slot + 16] += fold(new[...] - block_of(old, n, rows))


def new_shares(matrix, copies, out):
    out[...] = dot(matrix[...], copies[...].astype(BF16))


def squeeze(slot, log, *rest):
    *logs, out = rest
    values = log[...]
    out[...] = jnp.sum(values.reshape(-1, 8, values.shape[-1]), axis=1)
    tail = sum(part[...] for part in logs)
    out[slot // 8 : slot // 8 + 1] += jnp.sum(tail[:8], axis=0, keepdims=True)


def squeeze_last(slot, mine, got, *rest):
    *logs, out = rest
    tail = sum(part[...] for part in logs)
    out[...] = mine[...] + got[...]
    out[slot // 8 : slot // 8 + 1] += jnp.sum(tail[:8], axis=0, keepdims=True)
    out[slot // 8 + 1 : slot // 8 + 2] += jnp.sum(tail[8:], axis=0, keepdims=True)


def finish(devices, mine, got, cutoff, new, *kept):
    average = (mine[...] + got[...]) / devices
    clipped = jnp.clip(average, -cutoff[...], cutoff[...])
    new[...] = average - clipped
    for out in kept:
        out[...] = clipped


def merge(count, mine, got, log, out, log_out):
    out[...] = mine[...] + got[...]
    log_out[...] = log[...]
    log_out[...] += fold(mine[...] - got[...]) / (2 * count)


def finish_last(devices, mine, got, kept, old, cutoff, new, log_out):
    mean = (mine[...] + got[...]) / devices
    average = mean + kept[...]
    made = average - jnp.clip(average, -cutoff[...], cutoff[...])
    new[...] = made
    log_out[:8] = fold(mine[...] - got[...]) / devices + devices * fold(mean - made)
    log_out[8:] = devices * fold(made - old[...])


def reduce_block(part, order, index, size, log=None):
    for step, bit in enumerate(order[:-1]):
        low, high = jnp.split(part, 2, axis=0)
        upper = (index & bit) != 0
        got = swap(jnp.where(upper, low, high), "rows", size, bit)
        mine = jnp.where(upper, high, low)
        if log is None:
            part = mine + got
        else:
            part, log = call(
                functools.partial(merge, 2**step), [(mine.shape, F32), (log.shape, F32)], mine, got, log
            )
    return part, log


def gather_block(part, order, index, size):
    steps = order[-2::-1]
    for bit in steps:
        got = swap(part, "rows", size, bit)
        upper = (index & bit) != 0
        part = jnp.concatenate([jnp.where(upper, got, part), jnp.where(upper, part, got)], axis=0)
    return part


def trade_history(history, col_devices, row_devices):
    steps = [("cols", col_devices, bit) for bit in bits_of(col_devices)]
    steps += [("rows", row_devices, bit) for bit in bits_of(row_devices)[:-1]]
    for axis, size, bit in steps:
        got = swap(history, axis, size, bit)
        history = history + got
    return history


def local(matrix, inverse, target, penalty, consensus, copy_duals, fit_parts, fit_mean, fit_duals):
    row_devices = lax.axis_size("rows")
    col_devices = lax.axis_size("cols")
    index = lax.axis_index("rows")
    block_width, targets = consensus.shape
    height = matrix.shape[0]
    normalizer = float(row_devices * col_devices * block_width * targets)
    threshold = penalty / row_devices
    row_bits = bits_of(row_devices)
    turned = row_bits[1:2] + row_bits[:1] + row_bits[2:]
    orders = [row_bits if n % 2 == 0 else turned for n in range(STREAMS)]
    rows = block_width // STREAMS
    wide, tile, piece = (block_width, targets), (height, targets), (rows, targets)
    row_dual = fit_duals
    log = jnp.zeros((16 * ITERS, targets), F32)
    log_shape = (log.shape, F32)
    big = 2 * block_width * block_width * targets
    small = 2 * block_width * height * targets
    tall = matrix.T
    shares = fit_parts[0]
    total = shares + swap(shares, "cols", col_devices, 1)
    base = shares + (fit_mean - row_dual)
    for bit in bits_of(col_devices)[1:]:
        got = swap(total, "cols", col_devices, bit)
        total = total + got
    inverse = pl.pallas_call(
        stage,
        in_specs=[pl.BlockSpec(memory_space=pltpu.HBM)],
        out_shape=jax.ShapeDtypeStruct(inverse.shape, inverse.dtype),
        scratch_shapes=[pltpu.SemaphoreType.DMA],
        compiler_params=pltpu.CompilerParams(vmem_limit_bytes=40 * 1024 * 1024),
    )(inverse)
    centers, duals = [consensus] * STREAMS, [copy_duals[0]] * STREAMS
    (pulled,) = call(
        functools.partial(first_offsets, col_devices), [(wide, F32)], base, total, tall, flops=small
    )
    copies, *sums = call(
        first_copies, [(wide, F32)] + [(piece, F32)] * STREAMS, inverse, pulled, consensus, copy_duals[0],
        scratch=[pltpu.VMEM(wide, BF16)], flops=big,
    )
    owned, kept = [None] * STREAMS, [None] * STREAMS
    cutoff = threshold[None, :]
    for iteration in range(ITERS):
        slot = 16 * iteration
        last = iteration + 1 == ITERS
        plain = iteration + 2 == ITERS
        (shares,) = call(new_shares, [(tile, F32)], matrix, copies, flops=small)
        total = butterfly(shares, "cols", col_devices)
        if last:
            fitted, log = call(
                functools.partial(last_fit, col_devices, slot),
                [(tile, F32), log_shape], total, target, row_dual, log,
            )
        else:
            pulled, row_dual, log = call(
                functools.partial(next_offsets, col_devices, slot),
                [(wide, F32), (tile, F32), log_shape],
                shares, total, target, row_dual, tall, log, flops=small,
            )
        pairs = [
            reduce_block(sums[n], order, index, row_devices, jnp.zeros((8, targets), F32) if last else None)
            for n, order in enumerate(orders)
        ]
        partner = row_bits[-1]
        if last:
            (history,) = call(
                functools.partial(squeeze, slot), [((2 * ITERS, targets), F32)], log,
                *[pair[1] for pair in pairs],
            )
            early = swap(history, "rows", row_devices, partner)
        parts, logs = [], []
        for first in range(0, STREAMS, MERGED):
            group = range(first, first + MERGED)
            joined = jnp.concatenate([pairs[n][0] for n in group], axis=0)
            traded = swap(joined, "rows", row_devices, partner)
            traded = jnp.split(traded, MERGED, axis=0)
            for n, got in zip(group, traded):
                mine = pairs[n][0]
                shape = (mine.shape, F32)
                if last:
                    owned[n], tail = call(
                        functools.partial(finish_last, row_devices), [shape, ((16, targets), F32)],
                        mine, got, kept[n], owned[n], cutoff,
                    )
                    logs.append(tail)
                else:
                    made = call(
                        functools.partial(finish, row_devices), [shape] * (2 if plain else 1), mine, got, cutoff
                    )
                    owned[n], kept[n] = made[0], made[-1]
                parts.append(gather_block(owned[n], orders[n], index, row_devices))
        if last:
            (history,) = call(
                functools.partial(squeeze_last, slot), [((2 * ITERS, targets), F32)], history, early, *logs
            )
            history = trade_history(history, col_devices, row_devices)
            centers = parts
            break
        begun = []
        for n in range(STREAMS):
            final = n == STREAMS - 1
            made = call(
                functools.partial(update, n, slot, STREAMS, plain),
                [(piece, F32), log_shape, (wide, F32)] + [(piece, F32)] * (STREAMS if final else 0),
                inverse, parts[n], centers[n], copies, duals[n], pulled, log, *begun,
                *(duals[:-1] if final else []), flops=big // STREAMS,
            )
            duals[n], log, begun = made[0], made[1], [made[2]]
            sums = made[3:]
        centers = parts
        copies = begun[0]
    history = (jnp.sum(history, axis=1) / normalizer).reshape(ITERS, 2)
    return (jnp.concatenate(centers, axis=0), fitted, history)


def solution(mesh):
    in_specs = (
        P("rows", "cols"),
        P("rows", "cols"),
        P("rows", None),
        P(),
        P("cols", None),
        P("rows", "cols", None),
        P("cols", "rows", None),
        P("rows", None),
        P("rows", None),
    )
    out_specs = (P("cols", None), P("rows", None), P())
    return jax.shard_map(local, mesh=mesh, in_specs=in_specs, out_specs=out_specs, check_vma=False)
```

profile of v0, /device:TPU:0, one launch (start us, length us, event | category | flops | bytes accessed | tf_op | source)
XLA Modules:
  0.0 236.9 jit_solution(9674325163155618471)
XLA Ops:
  1.2 3.5 %shard_map.112.inverse = bf16[2048,2048]{1,0:T(8,128)(2,1)S(1)} custom-call(bf16[2048,2048]{1,0:T(8,128)(2,1)} %inverse.1), custom_call_target="tpu_custom_call" | custom-call | tf_op jit(solution)/shard_map/pallas_call | solution.py:226
  4.8 3.3 %copy-done = bf16[2048,2048]{1,0:T(8,128)(2,1)} copy-done((bf16[2048,2048]{1,0:T(8,128)(2,1)}, bf16[2048,2048]{1,0:T(8,128)(2,1)S(1)}, u32[]{:S(2)}) %copy-start) | copy-done | bytes 8388632
  10.4 2.6 %collective-permute-start.1 = (f32[256,128]{1,0:T(8,128)S(1)}, f32[256,128]{1,0:T(8,128)S(1)}, u32[]{:S(2)}, u32[]{:S(2)}) collective-permute-start(f32[256,128]{1,0:T(8,128)S(1)} %get-tuple-element.345), channel_id=1, source_target_pairs={{0,2},{1,3},{2,0},{3,1},{4,6},{5,7},{6,4},{7,5},{8,10},{9,11},{10,... | collective-permute-start | bytes 393224 | tf_op jit(solution)/shard_map/ppermute | solution.py:27
  13.0 4.1 %collective-permute-done.1 = f32[256,128]{1,0:T(8,128)S(1)} collective-permute-done((f32[256,128]{1,0:T(8,128)S(1)}, f32[256,128]{1,0:T(8,128)S(1)}, u32[]{:S(2)}, u32[]{:S(2)}) %collective-permute-start.1) | collective-permute-done | bytes 131104 | tf_op jit(solution)/shard_map/ppermute | solution.py:27
  18.8 3.4 %copy-done.1 = bf16[2048,2048]{1,0:T(8,128)(2,1)S(1)} copy-done((bf16[2048,2048]{1,0:T(8,128)(2,1)S(1)}, bf16[2048,2048]{1,0:T(8,128)(2,1)}, u32[]{:S(2)}) %copy-start.1) | copy-done | bytes 8388632
  22.2 2.4 %shard_map.114 = (f32[2048,128]{1,0:T(8,128)S(1)}, f32[512,128]{1,0:T(8,128)S(1)}, f32[512,128]{1,0:T(8,128)S(1)}, f32[512,128]{1,0:T(8,128)S(1)}, f32[512,128]{1,0:T(8,128)S(1)}) custom-call(bf16[2048,2048]{1,0:T(8,128)(2,1)S(1)} %copy-done.1, f32[2048,128]{1,0:T(8,128)S(1)} %shard_map.113.pulled, f32[2048,128]{1,0:T(8,128)S(1)} %copy-done.2, ...), custom_call_target="tpu_custom_call" | custom-call | flops 8589934592 | tf_op jit(solution)/shard_map/pallas_call | solution.py:46
  24.6 1.8 collective-permute-start.15
  31.7 2.1 collective-permute-start.14
  35.7 1.9 collective-permute-start.3
  37.6 2.7 %collective-permute-start.17 = (f32[256,128]{1,0:T(8,128)S(1)}, f32[256,128]{1,0:T(8,128)S(1)}, u32[]{:S(2)}, u32[]{:S(2)}) collective-permute-start(f32[256,128]{1,0:T(8,128)S(1)} %pad_maximum_fusion.19), channel_id=1, source_target_pairs={{0,16},{4,20},{8,24},{12,28},{16,0},{20,4},{24,8},{28,12},{1,17},{... | collective-permute-start | bytes 393224 | tf_op jit(solution)/shard_map/ppermute | solution.py:27
  40.3 2.4 %collective-permute-start.6 = (f32[256,128]{1,0:T(8,128)S(1)}, f32[256,128]{1,0:T(8,128)S(1)}, u32[]{:S(2)}, u32[]{:S(2)}) collective-permute-start(f32[256,128]{1,0:T(8,128)S(1)} %pad_maximum_fusion.16), channel_id=1, source_target_pairs={{0,16},{4,20},{8,24},{12,28},{16,0},{20,4},{24,8},{28,12},{1,17},{... | collective-permute-start | bytes 393224 | tf_op jit(solution)/shard_map/ppermute | solution.py:27
  43.2 5.9 %collective-permute-done.17 = f32[256,128]{1,0:T(8,128)S(1)} collective-permute-done((f32[256,128]{1,0:T(8,128)S(1)}, f32[256,128]{1,0:T(8,128)S(1)}, u32[]{:S(2)}, u32[]{:S(2)}) %collective-permute-start.17) | collective-permute-done | bytes 131104 | tf_op jit(solution)/shard_map/ppermute | solution.py:27
  50.7 1.8 collective-permute-start.11
  55.8 1.7 collective-permute-start.12
  66.3 1.7 collective-permute-start.33
  77.2 2.4 collective-permute-start.37
  80.0 2.9 %collective-permute-start.26 = (f32[256,128]{1,0:T(8,128)S(1)}, f32[256,128]{1,0:T(8,128)S(1)}, u32[]{:S(2)}, u32[]{:S(2)}) collective-permute-start(f32[256,128]{1,0:T(8,128)S(1)} %pad_maximum_fusion.22), channel_id=1, source_target_pairs={{0,16},{4,20},{8,24},{12,28},{16,0},{20,4},{24,8},{28,12},{1,17},{... | collective-permute-start | bytes 393224 | tf_op jit(solution)/shard_map/ppermute | solution.py:27
  83.4 5.7 %collective-permute-done.37 = f32[256,128]{1,0:T(8,128)S(1)} collective-permute-done((f32[256,128]{1,0:T(8,128)S(1)}, f32[256,128]{1,0:T(8,128)S(1)}, u32[]{:S(2)}, u32[]{:S(2)}) %collective-permute-start.37) | collective-permute-done | bytes 131104 | tf_op jit(solution)/shard_map/ppermute | solution.py:27
  117.0 2.3 collective-permute-start.57
  120.0 2.4 %collective-permute-start.46 = (f32[256,128]{1,0:T(8,128)S(1)}, f32[256,128]{1,0:T(8,128)S(1)}, u32[]{:S(2)}, u32[]{:S(2)}) collective-permute-start(f32[256,128]{1,0:T(8,128)S(1)} %pad_maximum_fusion.28), channel_id=1, source_target_pairs={{0,16},{4,20},{8,24},{12,28},{16,0},{20,4},{24,8},{28,12},{1,17},{... | collective-permute-start | bytes 393224 | tf_op jit(solution)/shard_map/ppermute | solution.py:27
  122.9 6.1 %collective-permute-done.57 = f32[256,128]{1,0:T(8,128)S(1)} collective-permute-done((f32[256,128]{1,0:T(8,128)S(1)}, f32[256,128]{1,0:T(8,128)S(1)}, u32[]{:S(2)}, u32[]{:S(2)}) %collective-permute-start.57) | collective-permute-done | bytes 131104 | tf_op jit(solution)/shard_map/ppermute | solution.py:27
  157.0 1.8 collective-permute-start.77
  160.1 1.8 collective-permute-start.66
  162.5 6.2 %collective-permute-done.77 = f32[256,128]{1,0:T(8,128)S(1)} collective-permute-done((f32[256,128]{1,0:T(8,128)S(1)}, f32[256,128]{1,0:T(8,128)S(1)}, u32[]{:S(2)}, u32[]{:S(2)}) %collective-permute-start.77) | collective-permute-done | bytes 131104 | tf_op jit(solution)/shard_map/ppermute | solution.py:27
  198.7 1.7 collective-permute-start.95
  201.8 1.7 collective-permute-start.86
  205.6 4.8 %collective-permute-done.95 = f32[256,128]{1,0:T(8,128)S(1)} collective-permute-done((f32[256,128]{1,0:T(8,128)S(1)}, f32[256,128]{1,0:T(8,128)S(1)}, u32[]{:S(2)}, u32[]{:S(2)}) %collective-permute-start.95) | collective-permute-done | bytes 131104 | tf_op jit(solution)/shard_map/ppermute | solution.py:27
  215.1 2.0 collective-permute-done.104
  218.2 2.7 %collective-permute-done.105 = f32[10,128]{1,0:T(8,128)S(1)} collective-permute-done((f32[10,128]{1,0:T(8,128)S(1)}, f32[10,128]{1,0:T(8,128)S(1)}, u32[]{:S(2)}, u32[]{:S(2)}) %collective-permute-start.105) | collective-permute-done | bytes 5152 | tf_op jit(solution)/shard_map/ppermute | solution.py:27
  221.8 2.0 collective-permute-start.96
  225.8 2.1 collective-permute-start.99
  231.4 3.3 %collective-permute-done.88 = f32[256,128]{1,0:T(8,128)S(1)} collective-permute-done((f32[256,128]{1,0:T(8,128)S(1)}, f32[256,128]{1,0:T(8,128)S(1)}, u32[]{:S(2)}, u32[]{:S(2)}) %collective-permute-start.88) | collective-permute-done | bytes 131104 | tf_op jit(solution)/shard_map/ppermute | solution.py:27
  (467 shorter events, 141.4 us)
Async XLA Ops:
  0.6 8.8 %collective-permute-start = (f32[256,128]{1,0:T(8,128)}, f32[256,128]{1,0:T(8,128)}, u32[]{:S(2)}, u32[]{:S(2)}) collective-permute-start(f32[256,128]{1,0:T(8,128)} %bitcast.19), channel_id=1, source_target_pairs={{0,1},{1,0},{2,3},{3,2},{4,5},{5,4},{6,7},{7,6},{8,9},{9,8},{10,11... | collective-permute-start | bytes 393224 | tf_op jit(solution)/shard_map/ppermute | solution.py:27
  10.4 6.7 %collective-permute-start.1 = (f32[256,128]{1,0:T(8,128)S(1)}, f32[256,128]{1,0:T(8,128)S(1)}, u32[]{:S(2)}, u32[]{:S(2)}) collective-permute-start(f32[256,128]{1,0:T(8,128)S(1)} %get-tuple-element.345), channel_id=1, source_target_pairs={{0,2},{1,3},{2,0},{3,1},{4,6},{5,7},{6,4},{7,5},{8,10},{9,11},{10,... | collective-permute-start | bytes 393224 | tf_op jit(solution)/shard_map/ppermute | solution.py:27
  28.7 6.5 %collective-permute-start.4 = (f32[256,128]{1,0:T(8,128)S(1)}, f32[256,128]{1,0:T(8,128)S(1)}, u32[]{:S(2)}, u32[]{:S(2)}) collective-permute-start(f32[256,128]{1,0:T(8,128)S(1)} %slice_select_fusion.22), channel_id=1, source_target_pairs={{0,4},{4,0},{8,12},{12,8},{16,20},{20,16},{24,28},{28,24},{1,5},{5... | collective-permute-start | bytes 393224 | tf_op jit(solution)/shard_map/ppermute | solution.py:27
  29.3 6.4 %collective-permute-start.2 = (f32[256,128]{1,0:T(8,128)S(1)}, f32[256,128]{1,0:T(8,128)S(1)}, u32[]{:S(2)}, u32[]{:S(2)}) collective-permute-start(f32[256,128]{1,0:T(8,128)S(1)} %slice_select_fusion.23), channel_id=1, source_target_pairs={{0,8},{4,12},{8,0},{12,4},{16,24},{20,28},{24,16},{28,20},{1,9},{5... | collective-permute-start | bytes 393224 | tf_op jit(solution)/shard_map/ppermute | solution.py:27
  30.0 7.5 %collective-permute-start.16 = (f32[128,128]{1,0:T(8,128)S(1)}, f32[128,128]{1,0:T(8,128)S(1)}, u32[]{:S(2)}, u32[]{:S(2)}) collective-permute-start(f32[128,128]{1,0:T(8,128)S(1)} %slice_select_fusion.36), channel_id=1, source_target_pairs={{0,8},{4,12},{8,0},{12,4},{16,24},{20,28},{24,16},{28,20},{1,9},{5... | collective-permute-start | bytes 196616 | tf_op jit(solution)/shard_map/ppermute | solution.py:27
  33.8 8.9 %collective-permute-start.10 = (f32[256,128]{1,0:T(8,128)S(1)}, f32[256,128]{1,0:T(8,128)S(1)}, u32[]{:S(2)}, u32[]{:S(2)}) collective-permute-start(f32[256,128]{1,0:T(8,128)S(1)} %add.154), channel_id=1, source_target_pairs={{0,2},{1,3},{2,0},{3,1},{4,6},{5,7},{6,4},{7,5},{8,10},{9,11},{10,... | collective-permute-start | bytes 393224 | tf_op jit(solution)/shard_map/ppermute | solution.py:27
  37.6 11.6 %collective-permute-start.17 = (f32[256,128]{1,0:T(8,128)S(1)}, f32[256,128]{1,0:T(8,128)S(1)}, u32[]{:S(2)}, u32[]{:S(2)}) collective-permute-start(f32[256,128]{1,0:T(8,128)S(1)} %pad_maximum_fusion.19), channel_id=1, source_target_pairs={{0,16},{4,20},{8,24},{12,28},{16,0},{20,4},{24,8},{28,12},{1,17},{... | collective-permute-start | bytes 393224 | tf_op jit(solution)/shard_map/ppermute | solution.py:27
  40.3 10.3 %collective-permute-start.6 = (f32[256,128]{1,0:T(8,128)S(1)}, f32[256,128]{1,0:T(8,128)S(1)}, u32[]{:S(2)}, u32[]{:S(2)}) collective-permute-start(f32[256,128]{1,0:T(8,128)S(1)} %pad_maximum_fusion.16), channel_id=1, source_target_pairs={{0,16},{4,20},{8,24},{12,28},{16,0},{20,4},{24,8},{28,12},{1,17},{... | collective-permute-start | bytes 393224 | tf_op jit(solution)/shard_map/ppermute | solution.py:27
  68.5 6.4 %collective-permute-start.24 = (f32[256,128]{1,0:T(8,128)S(1)}, f32[256,128]{1,0:T(8,128)S(1)}, u32[]{:S(2)}, u32[]{:S(2)}) collective-permute-start(f32[256,128]{1,0:T(8,128)S(1)} %slice_select_fusion.18), channel_id=1, source_target_pairs={{0,4},{4,0},{8,12},{12,8},{16,20},{20,16},{24,28},{28,24},{1,5},{5... | collective-permute-start | bytes 393224 | tf_op jit(solution)/shard_map/ppermute | solution.py:27
  69.2 6.4 %collective-permute-start.22 = (f32[256,128]{1,0:T(8,128)S(1)}, f32[256,128]{1,0:T(8,128)S(1)}, u32[]{:S(2)}, u32[]{:S(2)}) collective-permute-start(f32[256,128]{1,0:T(8,128)S(1)} %slice_select_fusion.19), channel_id=1, source_target_pairs={{0,8},{4,12},{8,0},{12,4},{16,24},{20,28},{24,16},{28,20},{1,9},{5... | collective-permute-start | bytes 393224 | tf_op jit(solution)/shard_map/ppermute | solution.py:27
  73.1 9.8 %collective-permute-start.30 = (f32[256,128]{1,0:T(8,128)S(1)}, f32[256,128]{1,0:T(8,128)S(1)}, u32[]{:S(2)}, u32[]{:S(2)}) collective-permute-start(f32[256,128]{1,0:T(8,128)S(1)} %add.164), channel_id=1, source_target_pairs={{0,2},{1,3},{2,0},{3,1},{4,6},{5,7},{6,4},{7,5},{8,10},{9,11},{10,... | collective-permute-start | bytes 393224 | tf_op jit(solution)/shard_map/ppermute | solution.py:27
  77.2 11.9 %collective-permute-start.37 = (f32[256,128]{1,0:T(8,128)S(1)}, f32[256,128]{1,0:T(8,128)S(1)}, u32[]{:S(2)}, u32[]{:S(2)}) collective-permute-start(f32[256,128]{1,0:T(8,128)S(1)} %pad_maximum_fusion.25), channel_id=1, source_target_pairs={{0,16},{4,20},{8,24},{12,28},{16,0},{20,4},{24,8},{28,12},{1,17},{... | collective-permute-start | bytes 393224 | tf_op jit(solution)/shard_map/ppermute | solution.py:27
  80.0 10.7 %collective-permute-start.26 = (f32[256,128]{1,0:T(8,128)S(1)}, f32[256,128]{1,0:T(8,128)S(1)}, u32[]{:S(2)}, u32[]{:S(2)}) collective-permute-start(f32[256,128]{1,0:T(8,128)S(1)} %pad_maximum_fusion.22), channel_id=1, source_target_pairs={{0,16},{4,20},{8,24},{12,28},{16,0},{20,4},{24,8},{28,12},{1,17},{... | collective-permute-start | bytes 393224 | tf_op jit(solution)/shard_map/ppermute | solution.py:27
  108.3 6.4 %collective-permute-start.44 = (f32[256,128]{1,0:T(8,128)S(1)}, f32[256,128]{1,0:T(8,128)S(1)}, u32[]{:S(2)}, u32[]{:S(2)}) collective-permute-start(f32[256,128]{1,0:T(8,128)S(1)} %slice_select_fusion.14), channel_id=1, source_target_pairs={{0,4},{4,0},{8,12},{12,8},{16,20},{20,16},{24,28},{28,24},{1,5},{5... | collective-permute-start | bytes 393224 | tf_op jit(solution)/shard_map/ppermute | solution.py:27
  112.9 9.5 %collective-permute-start.50 = (f32[256,128]{1,0:T(8,128)S(1)}, f32[256,128]{1,0:T(8,128)S(1)}, u32[]{:S(2)}, u32[]{:S(2)}) collective-permute-start(f32[256,128]{1,0:T(8,128)S(1)} %add.174), channel_id=1, source_target_pairs={{0,2},{1,3},{2,0},{3,1},{4,6},{5,7},{6,4},{7,5},{8,10},{9,11},{10,... | collective-permute-start | bytes 393224 | tf_op jit(solution)/shard_map/ppermute | solution.py:27
  117.0 12.0 %collective-permute-start.57 = (f32[256,128]{1,0:T(8,128)S(1)}, f32[256,128]{1,0:T(8,128)S(1)}, u32[]{:S(2)}, u32[]{:S(2)}) collective-permute-start(f32[256,128]{1,0:T(8,128)S(1)} %pad_maximum_fusion.31), channel_id=1, source_target_pairs={{0,16},{4,20},{8,24},{12,28},{16,0},{20,4},{24,8},{28,12},{1,17},{... | collective-permute-start | bytes 393224 | tf_op jit(solution)/shard_map/ppermute | solution.py:27
  120.0 10.6 %collective-permute-start.46 = (f32[256,128]{1,0:T(8,128)S(1)}, f32[256,128]{1,0:T(8,128)S(1)}, u32[]{:S(2)}, u32[]{:S(2)}) collective-permute-start(f32[256,128]{1,0:T(8,128)S(1)} %pad_maximum_fusion.28), channel_id=1, source_target_pairs={{0,16},{4,20},{8,24},{12,28},{16,0},{20,4},{24,8},{28,12},{1,17},{... | collective-permute-start | bytes 393224 | tf_op jit(solution)/shard_map/ppermute | solution.py:27
  149.3 6.4 %collective-permute-start.62 = (f32[256,128]{1,0:T(8,128)S(1)}, f32[256,128]{1,0:T(8,128)S(1)}, u32[]{:S(2)}, u32[]{:S(2)}) collective-permute-start(f32[256,128]{1,0:T(8,128)S(1)} %slice_select_fusion.11), channel_id=1, source_target_pairs={{0,8},{4,12},{8,0},{12,4},{16,24},{20,28},{24,16},{28,20},{1,9},{5... | collective-permute-start | bytes 393224 | tf_op jit(solution)/shard_map/ppermute | solution.py:27
  152.9 9.1 %collective-permute-start.70 = (f32[256,128]{1,0:T(8,128)S(1)}, f32[256,128]{1,0:T(8,128)S(1)}, u32[]{:S(2)}, u32[]{:S(2)}) collective-permute-start(f32[256,128]{1,0:T(8,128)S(1)} %add.184), channel_id=1, source_target_pairs={{0,2},{1,3},{2,0},{3,1},{4,6},{5,7},{6,4},{7,5},{8,10},{9,11},{10,... | collective-permute-start | bytes 393224 | tf_op jit(solution)/shard_map/ppermute | solution.py:27
  157.0 11.7 %collective-permute-start.77 = (f32[256,128]{1,0:T(8,128)S(1)}, f32[256,128]{1,0:T(8,128)S(1)}, u32[]{:S(2)}, u32[]{:S(2)}) collective-permute-start(f32[256,128]{1,0:T(8,128)S(1)} %pad_maximum_fusion.37), channel_id=1, source_target_pairs={{0,16},{4,20},{8,24},{12,28},{16,0},{20,4},{24,8},{28,12},{1,17},{... | collective-permute-start | bytes 393224 | tf_op jit(solution)/shard_map/ppermute | solution.py:27
  160.1 10.6 %collective-permute-start.66 = (f32[256,128]{1,0:T(8,128)S(1)}, f32[256,128]{1,0:T(8,128)S(1)}, u32[]{:S(2)}, u32[]{:S(2)}) collective-permute-start(f32[256,128]{1,0:T(8,128)S(1)} %pad_maximum_fusion.34), channel_id=1, source_target_pairs={{0,16},{4,20},{8,24},{12,28},{16,0},{20,4},{24,8},{28,12},{1,17},{... | collective-permute-start | bytes 393224 | tf_op jit(solution)/shard_map/ppermute | solution.py:27
  186.5 6.4 %collective-permute-start.93 = (f32[256,128]{1,0:T(8,128)S(1)}, f32[256,128]{1,0:T(8,128)S(1)}, u32[]{:S(2)}, u32[]{:S(2)}) collective-permute-start(f32[256,128]{1,0:T(8,128)S(1)} %get-tuple-element.237), channel_id=1, source_target_pairs={{0,8},{4,12},{8,0},{12,4},{16,24},{20,28},{24,16},{28,20},{1,9},{5... | collective-permute-start | bytes 393224 | tf_op jit(solution)/shard_map/ppermute | solution.py:27
  187.6 6.6 %collective-permute-start.91 = (f32[256,128]{1,0:T(8,128)S(1)}, f32[256,128]{1,0:T(8,128)S(1)}, u32[]{:S(2)}, u32[]{:S(2)}) collective-permute-start(f32[256,128]{1,0:T(8,128)S(1)} %get-tuple-element.239), channel_id=1, source_target_pairs={{0,4},{4,0},{8,12},{12,8},{16,20},{20,16},{24,28},{28,24},{1,5},{5... | collective-permute-start | bytes 393224 | tf_op jit(solution)/shard_map/ppermute | solution.py:27
  188.7 6.5 %collective-permute-start.84 = (f32[256,128]{1,0:T(8,128)S(1)}, f32[256,128]{1,0:T(8,128)S(1)}, u32[]{:S(2)}, u32[]{:S(2)}) collective-permute-start(f32[256,128]{1,0:T(8,128)S(1)} %get-tuple-element.241), channel_id=1, source_target_pairs={{0,8},{4,12},{8,0},{12,4},{16,24},{20,28},{24,16},{28,20},{1,9},{5... | collective-permute-start | bytes 393224 | tf_op jit(solution)/shard_map/ppermute | solution.py:27
  190.0 6.8 %collective-permute-start.82 = (f32[256,128]{1,0:T(8,128)S(1)}, f32[256,128]{1,0:T(8,128)S(1)}, u32[]{:S(2)}, u32[]{:S(2)}) collective-permute-start(f32[256,128]{1,0:T(8,128)S(1)} %get-tuple-element.243), channel_id=1, source_target_pairs={{0,4},{4,0},{8,12},{12,8},{16,20},{20,16},{24,28},{28,24},{1,5},{5... | collective-permute-start | bytes 393224 | tf_op jit(solution)/shard_map/ppermute | solution.py:27
  190.9 12.7 %collective-permute-start.101 = (f32[256,128]{1,0:T(8,128)S(1)}, f32[256,128]{1,0:T(8,128)S(1)}, u32[]{:S(2)}, u32[]{:S(2)}) collective-permute-start(f32[256,128]{1,0:T(8,128)S(1)} %add.190), channel_id=1, source_target_pairs={{0,2},{1,3},{2,0},{3,1},{4,6},{5,7},{6,4},{7,5},{8,10},{9,11},{10,... | collective-permute-start | bytes 393224 | tf_op jit(solution)/shard_map/ppermute | solution.py:27
  198.7 11.7 %collective-permute-start.95 = (f32[256,128]{1,0:T(8,128)S(1)}, f32[256,128]{1,0:T(8,128)S(1)}, u32[]{:S(2)}, u32[]{:S(2)}) collective-permute-start(f32[256,128]{1,0:T(8,128)S(1)} %pad_maximum_fusion.43), channel_id=1, source_target_pairs={{0,16},{4,20},{8,24},{12,28},{16,0},{20,4},{24,8},{28,12},{1,17},{... | collective-permute-start | bytes 393224 | tf_op jit(solution)/shard_map/ppermute | solution.py:27
  201.8 10.2 %collective-permute-start.86 = (f32[256,128]{1,0:T(8,128)S(1)}, f32[256,128]{1,0:T(8,128)S(1)}, u32[]{:S(2)}, u32[]{:S(2)}) collective-permute-start(f32[256,128]{1,0:T(8,128)S(1)} %pad_maximum_fusion.40), channel_id=1, source_target_pairs={{0,16},{4,20},{8,24},{12,28},{16,0},{20,4},{24,8},{28,12},{1,17},{... | collective-permute-start | bytes 393224 | tf_op jit(solution)/shard_map/ppermute | solution.py:27
  204.3 7.9 %collective-permute-start.102 = (f32[10,128]{1,0:T(8,128)S(1)}, f32[10,128]{1,0:T(8,128)S(1)}, u32[]{:S(2)}, u32[]{:S(2)}) collective-permute-start(f32[10,128]{1,0:T(8,128)S(1)} %shard_map.169.mine), channel_id=1, source_target_pairs={{0,16},{4,20},{8,24},{12,28},{16,0},{20,4},{24,8},{28,12},{1,17},{... | collective-permute-start | bytes 15368 | tf_op jit(solution)/shard_map/ppermute | solution.py:27
  223.8 6.9 %collective-permute-start.89 = (f32[128,128]{1,0:T(8,128)S(1)}, f32[128,128]{1,0:T(8,128)S(1)}, u32[]{:S(2)}, u32[]{:S(2)}) collective-permute-start(f32[128,128]{1,0:T(8,128)S(1)} %get-tuple-element.205), channel_id=1, source_target_pairs={{0,4},{4,0},{8,12},{12,8},{16,20},{20,16},{24,28},{28,24},{1,5},{5... | collective-permute-start | bytes 196616 | tf_op jit(solution)/shard_map/ppermute | solution.py:27
  225.8 10.1 %collective-permute-start.99 = (f32[256,128]{1,0:T(8,128)S(1)}, f32[256,128]{1,0:T(8,128)S(1)}, u32[]{:S(2)}, u32[]{:S(2)}) collective-permute-start(f32[256,128]{1,0:T(8,128)S(1)} %pad_maximum_fusion.45), channel_id=1, source_target_pairs={{0,8},{4,12},{8,0},{12,4},{16,24},{20,28},{24,16},{28,20},{1,9},{5... | collective-permute-start | bytes 393224 | tf_op jit(solution)/shard_map/ppermute | solution.py:27
  227.9 7.9 %collective-permute-start.97 = (f32[256,128]{1,0:T(8,128)S(1)}, f32[256,128]{1,0:T(8,128)S(1)}, u32[]{:S(2)}, u32[]{:S(2)}) collective-permute-start(f32[256,128]{1,0:T(8,128)S(1)} %pad_maximum_fusion.44), channel_id=1, source_target_pairs={{0,4},{4,0},{8,12},{12,8},{16,20},{20,16},{24,28},{28,24},{1,5},{5... | collective-permute-start | bytes 393224 | tf_op jit(solution)/shard_map/ppermute | solution.py:27
  (90 other events, 555.9 us)
where the time goes:
time: 237 us
  starting transfers between devices  123 us (52%)
  waiting for transfers between devices  71.7 us (30%)
  Pallas kernels  25.1 us (11%)
  local copies, waits for them, and re-layouts  11.1 us (5%)
  other arithmetic  3.68 us (2%)
    ppermute x107, starting transfers between devices, swap(): return lax.ppermute(values, axis, [(i, i ^ bit) for i in range(size)])  123 us
    ppermute x107, waiting for transfers between devices, swap(): return lax.ppermute(values, axis, [(i, i ^ bit) for i in range(size)])  71.7 us
    pallas_call x58, Pallas kernels, call(): pl.pallas_call(body, out_shape=[jax.ShapeDtypeStruct(s, d) for s, d in ou...  21.6 us
    unnamed x32, local copies, waits for them, and re-layouts  10.9 us
  transfers between devices with their start and end apart: 107, of which 52 were waited for; matrix products, arithmetic and copies ran while one was open for 2% of the time, Pallas kernels for 4%

commit v1 on v0

--- a/solution.py
+++ b/solution.py
@@ -25,12 +25,6 @@
 
 def swap(values, axis, size, bit):
     return lax.ppermute(values, axis, [(i, i ^ bit) for i in range(size)])
-
-
-def butterfly(values, axis, size):
-    for bit in bits_of(size):
-        values = values + swap(values, axis, size, bit)
-    return values
 
 
 def fold(values):
@@ -245,7 +239,10 @@
         last = iteration + 1 == ITERS
         plain = iteration + 2 == ITERS
         (shares,) = call(new_shares, [(tile, F32)], matrix, copies, flops=small)
-        total = butterfly(shares, "cols", col_devices)
+        total = shares
+        for bit in bits_of(col_devices):
+            got = swap(total, "cols", col_devices, bit)
+            total = total + got
         if last:
             fitted, log = call(
                 functools.partial(last_fit, col_devices, slot),

time: 237 us -> 237 us (level)
  no operation moved by 1% of the time
where the time goes in v1:
time: 237 us
  starting transfers between devices  123 us (52%)
  waiting for transfers between devices  71.7 us (30%)
  Pallas kernels  25.1 us (11%)
  local copies, waits for them, and re-layouts  11.1 us (5%)
  other arithmetic  3.68 us (2%)
    ppermute x107, starting transfers between devices, swap(): return lax.ppermute(values, axis, [(i, i ^ bit) for i in range(size)])  123 us
    ppermute x107, waiting for transfers between devices, swap(): return lax.ppermute(values, axis, [(i, i ^ bit) for i in range(size)])  71.7 us
    pallas_call x58, Pallas kernels, call(): pl.pallas_call(body, out_shape=[jax.ShapeDtypeStruct(s, d) for s, d in ou...  21.6 us
    unnamed x32, local copies, waits for them, and re-layouts  10.9 us
  transfers between devices with their start and end apart: 107, of which 52 were waited for; matrix products, arithmetic and copies ran while one was open for 2% of the time, Pallas kernels for 4%

profile of v1, /device:TPU:0, one launch (start us, length us, event | category | flops | bytes accessed | tf_op | source)
XLA Modules:
  0.0 236.9 jit_solution(9674325163155618471)
XLA Ops:
  1.2 3.5 %shard_map.112.inverse = bf16[2048,2048]{1,0:T(8,128)(2,1)S(1)} custom-call(bf16[2048,2048]{1,0:T(8,128)(2,1)} %inverse.1), custom_call_target="tpu_custom_call" | custom-call | tf_op jit(solution)/shard_map/pallas_call | solution.py:220
  4.8 3.3 %copy-done = bf16[2048,2048]{1,0:T(8,128)(2,1)} copy-done((bf16[2048,2048]{1,0:T(8,128)(2,1)}, bf16[2048,2048]{1,0:T(8,128)(2,1)S(1)}, u32[]{:S(2)}) %copy-start) | copy-done | bytes 8388632
  10.4 2.6 %collective-permute-start.1 = (f32[256,128]{1,0:T(8,128)S(1)}, f32[256,128]{1,0:T(8,128)S(1)}, u32[]{:S(2)}, u32[]{:S(2)}) collective-permute-start(f32[256,128]{1,0:T(8,128)S(1)} %get-tuple-element.345), channel_id=1, source_target_pairs={{0,2},{1,3},{2,0},{3,1},{4,6},{5,7},{6,4},{7,5},{8,10},{9,11},{10,... | collective-permute-start | bytes 393224 | tf_op jit(solution)/shard_map/ppermute | solution.py:27
  13.0 4.1 %collective-permute-done.1 = f32[256,128]{1,0:T(8,128)S(1)} collective-permute-done((f32[256,128]{1,0:T(8,128)S(1)}, f32[256,128]{1,0:T(8,128)S(1)}, u32[]{:S(2)}, u32[]{:S(2)}) %collective-permute-start.1) | collective-permute-done | bytes 131104 | tf_op jit(solution)/shard_map/ppermute | solution.py:27
  18.8 3.4 %copy-done.1 = bf16[2048,2048]{1,0:T(8,128)(2,1)S(1)} copy-done((bf16[2048,2048]{1,0:T(8,128)(2,1)S(1)}, bf16[2048,2048]{1,0:T(8,128)(2,1)}, u32[]{:S(2)}) %copy-start.1) | copy-done | bytes 8388632
  22.2 2.4 %shard_map.114 = (f32[2048,128]{1,0:T(8,128)S(1)}, f32[512,128]{1,0:T(8,128)S(1)}, f32[512,128]{1,0:T(8,128)S(1)}, f32[512,128]{1,0:T(8,128)S(1)}, f32[512,128]{1,0:T(8,128)S(1)}) custom-call(bf16[2048,2048]{1,0:T(8,128)(2,1)S(1)} %copy-done.1, f32[2048,128]{1,0:T(8,128)S(1)} %shard_map.113.pulled, f32[2048,128]{1,0:T(8,128)S(1)} %copy-done.2, ...), custom_call_target="tpu_custom_call" | custom-call | flops 8589934592 | tf_op jit(solution)/shard_map/pallas_call | solution.py:40
  24.6 1.8 collective-permute-start.15
  31.7 2.1 collective-permute-start.14
  35.7 1.9 collective-permute-start.3
  37.6 2.7 %collective-permute-start.17 = (f32[256,128]{1,0:T(8,128)S(1)}, f32[256,128]{1,0:T(8,128)S(1)}, u32[]{:S(2)}, u32[]{:S(2)}) collective-permute-start(f32[256,128]{1,0:T(8,128)S(1)} %pad_maximum_fusion.19), channel_id=1, source_target_pairs={{0,16},{4,20},{8,24},{12,28},{16,0},{20,4},{24,8},{28,12},{1,17},{... | collective-permute-start | bytes 393224 | tf_op jit(solution)/shard_map/ppermute | solution.py:27
  40.3 2.4 %collective-permute-start.6 = (f32[256,128]{1,0:T(8,128)S(1)}, f32[256,128]{1,0:T(8,128)S(1)}, u32[]{:S(2)}, u32[]{:S(2)}) collective-permute-start(f32[256,128]{1,0:T(8,128)S(1)} %pad_maximum_fusion.16), channel_id=1, source_target_pairs={{0,16},{4,20},{8,24},{12,28},{16,0},{20,4},{24,8},{28,12},{1,17},{... | collective-permute-start | bytes 393224 | tf_op jit(solution)/shard_map/ppermute | solution.py:27
  43.2 5.9 %collective-permute-done.17 = f32[256,128]{1,0:T(8,128)S(1)} collective-permute-done((f32[256,128]{1,0:T(8,128)S(1)}, f32[256,128]{1,0:T(8,128)S(1)}, u32[]{:S(2)}, u32[]{:S(2)}) %collective-permute-start.17) | collective-permute-done | bytes 131104 | tf_op jit(solution)/shard_map/ppermute | solution.py:27
  50.7 1.8 collective-permute-start.11
  55.8 1.7 collective-permute-start.12
  66.3 1.7 collective-permute-start.33
  77.2 2.4 collective-permute-start.37
  80.0 2.9 %collective-permute-start.26 = (f32[256,128]{1,0:T(8,128)S(1)}, f32[256,128]{1,0:T(8,128)S(1)}, u32[]{:S(2)}, u32[]{:S(2)}) collective-permute-start(f32[256,128]{1,0:T(8,128)S(1)} %pad_maximum_fusion.22), channel_id=1, source_target_pairs={{0,16},{4,20},{8,24},{12,28},{16,0},{20,4},{24,8},{28,12},{1,17},{... | collective-permute-start | bytes 393224 | tf_op jit(solution)/shard_map/ppermute | solution.py:27
  83.4 5.7 %collective-permute-done.37 = f32[256,128]{1,0:T(8,128)S(1)} collective-permute-done((f32[256,128]{1,0:T(8,128)S(1)}, f32[256,128]{1,0:T(8,128)S(1)}, u32[]{:S(2)}, u32[]{:S(2)}) %collective-permute-start.37) | collective-permute-done | bytes 131104 | tf_op jit(solution)/shard_map/ppermute | solution.py:27
  117.0 2.3 collective-permute-start.57
  120.0 2.4 %collective-permute-start.46 = (f32[256,128]{1,0:T(8,128)S(1)}, f32[256,128]{1,0:T(8,128)S(1)}, u32[]{:S(2)}, u32[]{:S(2)}) collective-permute-start(f32[256,128]{1,0:T(8,128)S(1)} %pad_maximum_fusion.28), channel_id=1, source_target_pairs={{0,16},{4,20},{8,24},{12,28},{16,0},{20,4},{24,8},{28,12},{1,17},{... | collective-permute-start | bytes 393224 | tf_op jit(solution)/shard_map/ppermute | solution.py:27
  122.9 6.1 %collective-permute-done.57 = f32[256,128]{1,0:T(8,128)S(1)} collective-permute-done((f32[256,128]{1,0:T(8,128)S(1)}, f32[256,128]{1,0:T(8,128)S(1)}, u32[]{:S(2)}, u32[]{:S(2)}) %collective-permute-start.57) | collective-permute-done | bytes 131104 | tf_op jit(solution)/shard_map/ppermute | solution.py:27
  157.0 1.8 collective-permute-start.77
  160.1 1.8 collective-permute-start.66
  162.5 6.2 %collective-permute-done.77 = f32[256,128]{1,0:T(8,128)S(1)} collective-permute-done((f32[256,128]{1,0:T(8,128)S(1)}, f32[256,128]{1,0:T(8,128)S(1)}, u32[]{:S(2)}, u32[]{:S(2)}) %collective-permute-start.77) | collective-permute-done | bytes 131104 | tf_op jit(solution)/shard_map/ppermute | solution.py:27
  198.7 1.7 collective-permute-start.95
  201.8 1.7 collective-permute-start.86
  205.6 4.8 %collective-permute-done.95 = f32[256,128]{1,0:T(8,128)S(1)} collective-permute-done((f32[256,128]{1,0:T(8,128)S(1)}, f32[256,128]{1,0:T(8,128)S(1)}, u32[]{:S(2)}, u32[]{:S(2)}) %collective-permute-start.95) | collective-permute-done | bytes 131104 | tf_op jit(solution)/shard_map/ppermute | solution.py:27
  215.1 2.0 collective-permute-done.104
  218.2 2.7 %collective-permute-done.105 = f32[10,128]{1,0:T(8,128)S(1)} collective-permute-done((f32[10,128]{1,0:T(8,128)S(1)}, f32[10,128]{1,0:T(8,128)S(1)}, u32[]{:S(2)}, u32[]{:S(2)}) %collective-permute-start.105) | collective-permute-done | bytes 5152 | tf_op jit(solution)/shard_map/ppermute | solution.py:27
  221.8 2.0 collective-permute-start.96
  225.8 2.1 collective-permute-start.99
  231.4 3.3 %collective-permute-done.88 = f32[256,128]{1,0:T(8,128)S(1)} collective-permute-done((f32[256,128]{1,0:T(8,128)S(1)}, f32[256,128]{1,0:T(8,128)S(1)}, u32[]{:S(2)}, u32[]{:S(2)}) %collective-permute-start.88) | collective-permute-done | bytes 131104 | tf_op jit(solution)/shard_map/ppermute | solution.py:27
  (467 shorter events, 141.4 us)
Async XLA Ops:
  0.6 8.8 %collective-permute-start = (f32[256,128]{1,0:T(8,128)}, f32[256,128]{1,0:T(8,128)}, u32[]{:S(2)}, u32[]{:S(2)}) collective-permute-start(f32[256,128]{1,0:T(8,128)} %bitcast.19), channel_id=1, source_target_pairs={{0,1},{1,0},{2,3},{3,2},{4,5},{5,4},{6,7},{7,6},{8,9},{9,8},{10,11... | collective-permute-start | bytes 393224 | tf_op jit(solution)/shard_map/ppermute | solution.py:27
  10.4 6.7 %collective-permute-start.1 = (f32[256,128]{1,0:T(8,128)S(1)}, f32[256,128]{1,0:T(8,128)S(1)}, u32[]{:S(2)}, u32[]{:S(2)}) collective-permute-start(f32[256,128]{1,0:T(8,128)S(1)} %get-tuple-element.345), channel_id=1, source_target_pairs={{0,2},{1,3},{2,0},{3,1},{4,6},{5,7},{6,4},{7,5},{8,10},{9,11},{10,... | collective-permute-start | bytes 393224 | tf_op jit(solution)/shard_map/ppermute | solution.py:27
  28.7 6.5 %collective-permute-start.4 = (f32[256,128]{1,0:T(8,128)S(1)}, f32[256,128]{1,0:T(8,128)S(1)}, u32[]{:S(2)}, u32[]{:S(2)}) collective-permute-start(f32[256,128]{1,0:T(8,128)S(1)} %slice_select_fusion.22), channel_id=1, source_target_pairs={{0,4},{4,0},{8,12},{12,8},{16,20},{20,16},{24,28},{28,24},{1,5},{5... | collective-permute-start | bytes 393224 | tf_op jit(solution)/shard_map/ppermute | solution.py:27
  29.3 6.4 %collective-permute-start.2 = (f32[256,128]{1,0:T(8,128)S(1)}, f32[256,128]{1,0:T(8,128)S(1)}, u32[]{:S(2)}, u32[]{:S(2)}) collective-permute-start(f32[256,128]{1,0:T(8,128)S(1)} %slice_select_fusion.23), channel_id=1, source_target_pairs={{0,8},{4,12},{8,0},{12,4},{16,24},{20,28},{24,16},{28,20},{1,9},{5... | collective-permute-start | bytes 393224 | tf_op jit(solution)/shard_map/ppermute | solution.py:27
  30.0 7.5 %collective-permute-start.16 = (f32[128,128]{1,0:T(8,128)S(1)}, f32[128,128]{1,0:T(8,128)S(1)}, u32[]{:S(2)}, u32[]{:S(2)}) collective-permute-start(f32[128,128]{1,0:T(8,128)S(1)} %slice_select_fusion.36), channel_id=1, source_target_pairs={{0,8},{4,12},{8,0},{12,4},{16,24},{20,28},{24,16},{28,20},{1,9},{5... | collective-permute-start | bytes 196616 | tf_op jit(solution)/shard_map/ppermute | solution.py:27
  33.8 8.9 %collective-permute-start.10 = (f32[256,128]{1,0:T(8,128)S(1)}, f32[256,128]{1,0:T(8,128)S(1)}, u32[]{:S(2)}, u32[]{:S(2)}) collective-permute-start(f32[256,128]{1,0:T(8,128)S(1)} %add.154), channel_id=1, source_target_pairs={{0,2},{1,3},{2,0},{3,1},{4,6},{5,7},{6,4},{7,5},{8,10},{9,11},{10,... | collective-permute-start | bytes 393224 | tf_op jit(solution)/shard_map/ppermute | solution.py:27
  37.6 11.6 %collective-permute-start.17 = (f32[256,128]{1,0:T(8,128)S(1)}, f32[256,128]{1,0:T(8,128)S(1)}, u32[]{:S(2)}, u32[]{:S(2)}) collective-permute-start(f32[256,128]{1,0:T(8,128)S(1)} %pad_maximum_fusion.19), channel_id=1, source_target_pairs={{0,16},{4,20},{8,24},{12,28},{16,0},{20,4},{24,8},{28,12},{1,17},{... | collective-permute-start | bytes 393224 | tf_op jit(solution)/shard_map/ppermute | solution.py:27
  40.3 10.3 %collective-permute-start.6 = (f32[256,128]{1,0:T(8,128)S(1)}, f32[256,128]{1,0:T(8,128)S(1)}, u32[]{:S(2)}, u32[]{:S(2)}) collective-permute-start(f32[256,128]{1,0:T(8,128)S(1)} %pad_maximum_fusion.16), channel_id=1, source_target_pairs={{0,16},{4,20},{8,24},{12,28},{16,0},{20,4},{24,8},{28,12},{1,17},{... | collective-permute-start | bytes 393224 | tf_op jit(solution)/shard_map/ppermute | solution.py:27
  68.5 6.4 %collective-permute-start.24 = (f32[256,128]{1,0:T(8,128)S(1)}, f32[256,128]{1,0:T(8,128)S(1)}, u32[]{:S(2)}, u32[]{:S(2)}) collective-permute-start(f32[256,128]{1,0:T(8,128)S(1)} %slice_select_fusion.18), channel_id=1, source_target_pairs={{0,4},{4,0},{8,12},{12,8},{16,20},{20,16},{24,28},{28,24},{1,5},{5... | collective-permute-start | bytes 393224 | tf_op jit(solution)/shard_map/ppermute | solution.py:27
  69.2 6.4 %collective-permute-start.22 = (f32[256,128]{1,0:T(8,128)S(1)}, f32[256,128]{1,0:T(8,128)S(1)}, u32[]{:S(2)}, u32[]{:S(2)}) collective-permute-start(f32[256,128]{1,0:T(8,128)S(1)} %slice_select_fusion.19), channel_id=1, source_target_pairs={{0,8},{4,12},{8,0},{12,4},{16,24},{20,28},{24,16},{28,20},{1,9},{5... | collective-permute-start | bytes 393224 | tf_op jit(solution)/shard_map/ppermute | solution.py:27
  73.1 9.8 %collective-permute-start.30 = (f32[256,128]{1,0:T(8,128)S(1)}, f32[256,128]{1,0:T(8,128)S(1)}, u32[]{:S(2)}, u32[]{:S(2)}) collective-permute-start(f32[256,128]{1,0:T(8,128)S(1)} %add.164), channel_id=1, source_target_pairs={{0,2},{1,3},{2,0},{3,1},{4,6},{5,7},{6,4},{7,5},{8,10},{9,11},{10,... | collective-permute-start | bytes 393224 | tf_op jit(solution)/shard_map/ppermute | solution.py:27
  77.2 11.9 %collective-permute-start.37 = (f32[256,128]{1,0:T(8,128)S(1)}, f32[256,128]{1,0:T(8,128)S(1)}, u32[]{:S(2)}, u32[]{:S(2)}) collective-permute-start(f32[256,128]{1,0:T(8,128)S(1)} %pad_maximum_fusion.25), channel_id=1, source_target_pairs={{0,16},{4,20},{8,24},{12,28},{16,0},{20,4},{24,8},{28,12},{1,17},{... | collective-permute-start | bytes 393224 | tf_op jit(solution)/shard_map/ppermute | solution.py:27
  80.0 10.7 %collective-permute-start.26 = (f32[256,128]{1,0:T(8,128)S(1)}, f32[256,128]{1,0:T(8,128)S(1)}, u32[]{:S(2)}, u32[]{:S(2)}) collective-permute-start(f32[256,128]{1,0:T(8,128)S(1)} %pad_maximum_fusion.22), channel_id=1, source_target_pairs={{0,16},{4,20},{8,24},{12,28},{16,0},{20,4},{24,8},{28,12},{1,17},{... | collective-permute-start | bytes 393224 | tf_op jit(solution)/shard_map/ppermute | solution.py:27
  108.3 6.4 %collective-permute-start.44 = (f32[256,128]{1,0:T(8,128)S(1)}, f32[256,128]{1,0:T(8,128)S(1)}, u32[]{:S(2)}, u32[]{:S(2)}) collective-permute-start(f32[256,128]{1,0:T(8,128)S(1)} %slice_select_fusion.14), channel_id=1, source_target_pairs={{0,4},{4,0},{8,12},{12,8},{16,20},{20,16},{24,28},{28,24},{1,5},{5... | collective-permute-start | bytes 393224 | tf_op jit(solution)/shard_map/ppermute | solution.py:27
  112.9 9.5 %collective-permute-start.50 = (f32[256,128]{1,0:T(8,128)S(1)}, f32[256,128]{1,0:T(8,128)S(1)}, u32[]{:S(2)}, u32[]{:S(2)}) collective-permute-start(f32[256,128]{1,0:T(8,128)S(1)} %add.174), channel_id=1, source_target_pairs={{0,2},{1,3},{2,0},{3,1},{4,6},{5,7},{6,4},{7,5},{8,10},{9,11},{10,... | collective-permute-start | bytes 393224 | tf_op jit(solution)/shard_map/ppermute | solution.py:27
  117.0 12.0 %collective-permute-start.57 = (f32[256,128]{1,0:T(8,128)S(1)}, f32[256,128]{1,0:T(8,128)S(1)}, u32[]{:S(2)}, u32[]{:S(2)}) collective-permute-start(f32[256,128]{1,0:T(8,128)S(1)} %pad_maximum_fusion.31), channel_id=1, source_target_pairs={{0,16},{4,20},{8,24},{12,28},{16,0},{20,4},{24,8},{28,12},{1,17},{... | collective-permute-start | bytes 393224 | tf_op jit(solution)/shard_map/ppermute | solution.py:27
  120.0 10.6 %collective-permute-start.46 = (f32[256,128]{1,0:T(8,128)S(1)}, f32[256,128]{1,0:T(8,128)S(1)}, u32[]{:S(2)}, u32[]{:S(2)}) collective-permute-start(f32[256,128]{1,0:T(8,128)S(1)} %pad_maximum_fusion.28), channel_id=1, source_target_pairs={{0,16},{4,20},{8,24},{12,28},{16,0},{20,4},{24,8},{28,12},{1,17},{... | collective-permute-start | bytes 393224 | tf_op jit(solution)/shard_map/ppermute | solution.py:27
  149.3 6.4 %collective-permute-start.62 = (f32[256,128]{1,0:T(8,128)S(1)}, f32[256,128]{1,0:T(8,128)S(1)}, u32[]{:S(2)}, u32[]{:S(2)}) collective-permute-start(f32[256,128]{1,0:T(8,128)S(1)} %slice_select_fusion.11), channel_id=1, source_target_pairs={{0,8},{4,12},{8,0},{12,4},{16,24},{20,28},{24,16},{28,20},{1,9},{5... | collective-permute-start | bytes 393224 | tf_op jit(solution)/shard_map/ppermute | solution.py:27
  152.9 9.1 %collective-permute-start.70 = (f32[256,128]{1,0:T(8,128)S(1)}, f32[256,128]{1,0:T(8,128)S(1)}, u32[]{:S(2)}, u32[]{:S(2)}) collective-permute-start(f32[256,128]{1,0:T(8,128)S(1)} %add.184), channel_id=1, source_target_pairs={{0,2},{1,3},{2,0},{3,1},{4,6},{5,7},{6,4},{7,5},{8,10},{9,11},{10,... | collective-permute-start | bytes 393224 | tf_op jit(solution)/shard_map/ppermute | solution.py:27
  157.0 11.7 %collective-permute-start.77 = (f32[256,128]{1,0:T(8,128)S(1)}, f32[256,128]{1,0:T(8,128)S(1)}, u32[]{:S(2)}, u32[]{:S(2)}) collective-permute-start(f32[256,128]{1,0:T(8,128)S(1)} %pad_maximum_fusion.37), channel_id=1, source_target_pairs={{0,16},{4,20},{8,24},{12,28},{16,0},{20,4},{24,8},{28,12},{1,17},{... | collective-permute-start | bytes 393224 | tf_op jit(solution)/shard_map/ppermute | solution.py:27
  160.1 10.6 %collective-permute-start.66 = (f32[256,128]{1,0:T(8,128)S(1)}, f32[256,128]{1,0:T(8,128)S(1)}, u32[]{:S(2)}, u32[]{:S(2)}) collective-permute-start(f32[256,128]{1,0:T(8,128)S(1)} %pad_maximum_fusion.34), channel_id=1, source_target_pairs={{0,16},{4,20},{8,24},{12,28},{16,0},{20,4},{24,8},{28,12},{1,17},{... | collective-permute-start | bytes 393224 | tf_op jit(solution)/shard_map/ppermute | solution.py:27
  186.5 6.4 %collective-permute-start.93 = (f32[256,128]{1,0:T(8,128)S(1)}, f32[256,128]{1,0:T(8,128)S(1)}, u32[]{:S(2)}, u32[]{:S(2)}) collective-permute-start(f32[256,128]{1,0:T(8,128)S(1)} %get-tuple-element.237), channel_id=1, source_target_pairs={{0,8},{4,12},{8,0},{12,4},{16,24},{20,28},{24,16},{28,20},{1,9},{5... | collective-permute-start | bytes 393224 | tf_op jit(solution)/shard_map/ppermute | solution.py:27
  187.6 6.6 %collective-permute-start.91 = (f32[256,128]{1,0:T(8,128)S(1)}, f32[256,128]{1,0:T(8,128)S(1)}, u32[]{:S(2)}, u32[]{:S(2)}) collective-permute-start(f32[256,128]{1,0:T(8,128)S(1)} %get-tuple-element.239), channel_id=1, source_target_pairs={{0,4},{4,0},{8,12},{12,8},{16,20},{20,16},{24,28},{28,24},{1,5},{5... | collective-permute-start | bytes 393224 | tf_op jit(solution)/shard_map/ppermute | solution.py:27
  188.7 6.5 %collective-permute-start.84 = (f32[256,128]{1,0:T(8,128)S(1)}, f32[256,128]{1,0:T(8,128)S(1)}, u32[]{:S(2)}, u32[]{:S(2)}) collective-permute-start(f32[256,128]{1,0:T(8,128)S(1)} %get-tuple-element.241), channel_id=1, source_target_pairs={{0,8},{4,12},{8,0},{12,4},{16,24},{20,28},{24,16},{28,20},{1,9},{5... | collective-permute-start | bytes 393224 | tf_op jit(solution)/shard_map/ppermute | solution.py:27
  190.0 6.8 %collective-permute-start.82 = (f32[256,128]{1,0:T(8,128)S(1)}, f32[256,128]{1,0:T(8,128)S(1)}, u32[]{:S(2)}, u32[]{:S(2)}) collective-permute-start(f32[256,128]{1,0:T(8,128)S(1)} %get-tuple-element.243), channel_id=1, source_target_pairs={{0,4},{4,0},{8,12},{12,8},{16,20},{20,16},{24,28},{28,24},{1,5},{5... | collective-permute-start | bytes 393224 | tf_op jit(solution)/shard_map/ppermute | solution.py:27
  190.9 12.7 %collective-permute-start.101 = (f32[256,128]{1,0:T(8,128)S(1)}, f32[256,128]{1,0:T(8,128)S(1)}, u32[]{:S(2)}, u32[]{:S(2)}) collective-permute-start(f32[256,128]{1,0:T(8,128)S(1)} %add.190), channel_id=1, source_target_pairs={{0,2},{1,3},{2,0},{3,1},{4,6},{5,7},{6,4},{7,5},{8,10},{9,11},{10,... | collective-permute-start | bytes 393224 | tf_op jit(solution)/shard_map/ppermute | solution.py:27
  198.7 11.7 %collective-permute-start.95 = (f32[256,128]{1,0:T(8,128)S(1)}, f32[256,128]{1,0:T(8,128)S(1)}, u32[]{:S(2)}, u32[]{:S(2)}) collective-permute-start(f32[256,128]{1,0:T(8,128)S(1)} %pad_maximum_fusion.43), channel_id=1, source_target_pairs={{0,16},{4,20},{8,24},{12,28},{16,0},{20,4},{24,8},{28,12},{1,17},{... | collective-permute-start | bytes 393224 | tf_op jit(solution)/shard_map/ppermute | solution.py:27
  201.8 10.2 %collective-permute-start.86 = (f32[256,128]{1,0:T(8,128)S(1)}, f32[256,128]{1,0:T(8,128)S(1)}, u32[]{:S(2)}, u32[]{:S(2)}) collective-permute-start(f32[256,128]{1,0:T(8,128)S(1)} %pad_maximum_fusion.40), channel_id=1, source_target_pairs={{0,16},{4,20},{8,24},{12,28},{16,0},{20,4},{24,8},{28,12},{1,17},{... | collective-permute-start | bytes 393224 | tf_op jit(solution)/shard_map/ppermute | solution.py:27
  204.3 7.9 %collective-permute-start.102 = (f32[10,128]{1,0:T(8,128)S(1)}, f32[10,128]{1,0:T(8,128)S(1)}, u32[]{:S(2)}, u32[]{:S(2)}) collective-permute-start(f32[10,128]{1,0:T(8,128)S(1)} %shard_map.169.mine), channel_id=1, source_target_pairs={{0,16},{4,20},{8,24},{12,28},{16,0},{20,4},{24,8},{28,12},{1,17},{... | collective-permute-start | bytes 15368 | tf_op jit(solution)/shard_map/ppermute | solution.py:27
  223.8 6.9 %collective-permute-start.89 = (f32[128,128]{1,0:T(8,128)S(1)}, f32[128,128]{1,0:T(8,128)S(1)}, u32[]{:S(2)}, u32[]{:S(2)}) collective-permute-start(f32[128,128]{1,0:T(8,128)S(1)} %get-tuple-element.205), channel_id=1, source_target_pairs={{0,4},{4,0},{8,12},{12,8},{16,20},{20,16},{24,28},{28,24},{1,5},{5... | collective-permute-start | bytes 196616 | tf_op jit(solution)/shard_map/ppermute | solution.py:27
  225.8 10.1 %collective-permute-start.99 = (f32[256,128]{1,0:T(8,128)S(1)}, f32[256,128]{1,0:T(8,128)S(1)}, u32[]{:S(2)}, u32[]{:S(2)}) collective-permute-start(f32[256,128]{1,0:T(8,128)S(1)} %pad_maximum_fusion.45), channel_id=1, source_target_pairs={{0,8},{4,12},{8,0},{12,4},{16,24},{20,28},{24,16},{28,20},{1,9},{5... | collective-permute-start | bytes 393224 | tf_op jit(solution)/shard_map/ppermute | solution.py:27
  227.9 7.9 %collective-permute-start.97 = (f32[256,128]{1,0:T(8,128)S(1)}, f32[256,128]{1,0:T(8,128)S(1)}, u32[]{:S(2)}, u32[]{:S(2)}) collective-permute-start(f32[256,128]{1,0:T(8,128)S(1)} %pad_maximum_fusion.44), channel_id=1, source_target_pairs={{0,4},{4,0},{8,12},{12,8},{16,20},{20,16},{24,28},{28,24},{1,5},{5... | collective-permute-start | bytes 393224 | tf_op jit(solution)/shard_map/ppermute | solution.py:27
  (90 other events, 555.9 us)
